TPU v7x, 128 devices: a whole 4x4x4 slice. The times are simulated.
128 devices in a mesh: row: 8 (over y, core), col: 16 (over z, x).
Axes of the slice: x: 4, y: 4, z: 4, core: 2. Of those that a mesh axis runs over, the one named last changes fastest.
Arguments:
- current_left: bfloat16 [8, 256, 768, 128], P('row', 'col'), may hold values from -6 to 6
- current_right: bfloat16 [8, 256, 768, 128], P('row', 'col'), may hold values from -0.21875 to 0.21875
- current_rank: int32 [8, 256], P('row', 'col'), may hold values from 1 to 128
- target_rank: int32 [8, 256], P('row', 'col'), may hold values from 1 to 128
- update_left: bfloat16 [8, 128, 768, 128], P('row', 'col'), may hold values from -6 to 6
- update_right: bfloat16 [8, 128, 768, 128], P('row', 'col'), may hold values from -0.21875 to 0.21875
- update_rank: int32 [8, 128], P('row', 'col'), may hold values from 1 to 128
- owner_slot: int32 [8, 128], P('row', 'col'), may hold values from 0 to 255, as said below
Outputs:
- compressed_left: bfloat16 [8, 256, 768, 128], P('row', 'col')
- returned_right: bfloat16 [8, 128, 768, 128], P('row', 'col')
- row_scale: float32 [16, 768], P('row')
Inputs may be any that keep to these rules, and one draw needn't show every extreme that they name: `owner_slot`: an entry is the tile's owning column index times 16 plus the tile's place on that owner. No tile is named by two contributions of its grid row. One device names either none or exactly 2 tiles of each owner. In every grid row some owner has all of its 16 tiles named.
All inputs are finite; a program needn't handle non-finite values.
Results may differ from a plain program's by a relative error of at most 0.0085.
Values may be sent and summed in bfloat16 or wider, within the bound.
No kernel may reach another device: no remote copies, remote signals or barrier semaphores. Data moves between devices by JAX's collectives and lax.ppermute only.
A program may use at most 128 MiB of HBM per device.

v0:
```python
import math

import jax
import jax.numpy as jnp
from jax import lax
from jax.sharding import PartitionSpec as P

CAP = 2
BR = 2
SWEEPS = 8
ROOTS = 3


def in_one_piece(arrays, axis, split_dim, concat_dim, along):
    both = jnp.concatenate(arrays, axis=along)
    filled, at, done = (
        lax.all_to_all(both, axis, split_axis=split_dim, concat_axis=concat_dim, tiled=True),
        0,
        [],
    )
    for a in arrays:
        done.append(lax.slice_in_dim(filled, at, at + a.shape[along], axis=along))
        at += a.shape[along]
    return tuple(done)


def split_up(value, dim, length):
    before, after = (value.shape[:dim], value.shape[dim + 1 :])
    return jnp.moveaxis(value.reshape(*before, length, -1, *after), dim, 0)


def piece_ends(length, count):
    unit = 8 if length >= 8 * count else 1
    return [length // unit * k // count * unit for k in range(1, count)]


def joined_along(pieces, dim):
    shape = list(pieces.shape[1:])
    shape[dim] *= pieces.shape[0]
    return jnp.moveaxis(pieces, 0, dim).reshape(shape)


def exchange_in_pieces(value, axis, pieces, split_dim, concat_dim):
    blocks = split_up(value, split_dim, lax.axis_size(axis))
    widest = max(range(1, max(2, blocks.ndim - 1)), key=lambda d: blocks.shape[d])
    done = []
    for slab in jnp.split(blocks, piece_ends(blocks.shape[widest], pieces), axis=widest):
        if slab.size:
            done.append(lax.all_to_all(slab, axis, split_axis=0, concat_axis=0, tiled=True))
    return joined_along(jnp.concatenate(done, axis=widest), concat_dim)


def copy_for_each(value, axis):
    copies = jnp.broadcast_to(value, (lax.axis_size(axis), *value.shape))
    return lax.all_to_all(copies, axis, split_axis=0, concat_axis=0, tiled=True)


def taken_together(value, axis):
    everything = copy_for_each(value, axis)
    return jnp.sum(everything, axis=0)


def high_dot(first, second):
    return jnp.dot(first, second, precision=lax.Precision.HIGHEST)


def gram_of(stacked):
    return lax.dot_general(
        stacked, stacked, (((0,), (0,)), ((), ())), preferred_element_type=jnp.float32
    )


def split_product(stacked, small):
    upper_part = small.astype(jnp.bfloat16)
    lower_part = (small - upper_part.astype(jnp.float32)).astype(jnp.bfloat16)
    first = jnp.dot(stacked, upper_part, preferred_element_type=jnp.float32)
    return first + jnp.dot(stacked, lower_part, preferred_element_type=jnp.float32)


def square_roots(gram):
    order = gram.shape[0]
    identity = jnp.eye(order, dtype=jnp.float32)
    scale_value = jnp.sqrt(jnp.sum(gram * gram))
    root_now = gram / scale_value
    inverse_now = identity
    for repeat in range(ROOTS):
        middle = 1.5 * identity - 0.5 * high_dot(inverse_now, root_now)
        root_now = high_dot(root_now, middle)
        inverse_now = high_dot(middle, inverse_now)
    return (root_now * jnp.sqrt(scale_value), inverse_now / jnp.sqrt(scale_value))


def recompress(old_left, old_right, old_rank, add_left, add_right, add_rank, keep_rank):
    half_width = old_left.shape[1]
    column = jnp.arange(2 * half_width)
    live_mask = jnp.where(
        column < half_width, column < old_rank, column - half_width < add_rank
    ).astype(jnp.float32)
    live_narrow = live_mask.astype(jnp.bfloat16)
    stack_left = jnp.concatenate([old_left, add_left], axis=1) * live_narrow
    stack_right = jnp.concatenate([old_right, add_right], axis=1) * live_narrow
    gram_left = gram_of(stack_left)
    gram_right = gram_of(stack_right) + jnp.diag(1.0 - live_mask)
    root_factor, inverse_factor = square_roots(gram_right)
    core_matrix = high_dot(high_dot(root_factor, gram_left), root_factor)
    subspace = core_matrix[:, :half_width] + core_matrix[:, half_width:]
    subspace = subspace / jnp.sqrt(jnp.sum(subspace * subspace) + 1e-06)
    for repeat in range(SWEEPS):
        inner = high_dot(subspace.T, subspace)
        subspace = 1.5 * subspace - 0.5 * high_dot(subspace, inner)
    subspace_kept = subspace * (jnp.arange(half_width) < keep_rank).astype(jnp.float32)
    new_left = split_product(stack_left, high_dot(root_factor, subspace_kept))
    solved = high_dot(inverse_factor, subspace_kept)
    new_right = split_product(stack_right, solved) * math.sqrt(stack_right.shape[0])
    return (new_left.astype(jnp.bfloat16), new_right.astype(jnp.bfloat16))


def route_table(owner_slot, tile_count, peer_count):
    destination = owner_slot // tile_count
    local_tile = owner_slot % tile_count
    slot_order = jnp.arange(owner_slot.shape[0])
    same_owner = (destination[:, None] == destination[None, :]) & (
        slot_order[None, :] < slot_order[:, None]
    )
    buffer_place = destination * CAP + jnp.sum(same_owner.astype(jnp.int32), axis=1)
    positions = jnp.arange(peer_count * CAP)
    chosen = buffer_place[None, :] == positions[:, None]
    filled = jnp.any(chosen, axis=1)
    source_slot = jnp.sum(jnp.where(chosen, slot_order[None, :], 0), axis=1)
    return (local_tile, buffer_place, filled, source_slot)


def pack_rows(values, filled, source_slot, peer_count):
    picked = jnp.take(values, source_slot, axis=0)
    shaped_mask = filled.reshape((-1,) + (1,) * (values.ndim - 1))
    packed = jnp.where(shaped_mask, picked, jnp.zeros((), values.dtype))
    return packed.reshape((peer_count, CAP) + values.shape[1:])


def match_tiles(arrived_tile, tile_count):
    matched = arrived_tile[None, :] == jnp.arange(tile_count)[:, None]
    tile_hit = jnp.any(matched, axis=1)
    arrival_index = jnp.sum(
        jnp.where(matched, jnp.arange(arrived_tile.shape[0])[None, :], 0), axis=1
    )
    return (tile_hit, arrival_index)


def flatten_peers(values):
    return values.reshape((values.shape[0] * values.shape[1],) + values.shape[2:])


def local(
    current_left,
    current_right,
    current_rank,
    target_rank,
    update_left,
    update_right,
    update_rank,
    owner_slot,
):
    peer_count = lax.axis_size("col")
    tile_count = current_left.shape[1]
    own_left = current_left[0]
    own_right = current_right[0]
    own_rank = current_rank[0]
    own_target = target_rank[0]
    local_tile, buffer_place, filled, source_slot = route_table(
        owner_slot[0], tile_count, peer_count
    )
    tile_buffer = jnp.where(filled, jnp.take(local_tile, source_slot), tile_count).reshape(
        peer_count, CAP
    )
    keep_cols = jnp.arange(own_left.shape[2]) < own_rank[:, None]
    masked_left = jnp.where(keep_cols[:, None, :], own_left, jnp.zeros((), own_left.dtype))
    asked_tile = flatten_peers(
        lax.all_to_all(tile_buffer, "col", split_axis=0, concat_axis=0, tiled=True)
    )
    asked_used = asked_tile < tile_count
    asked_safe = jnp.minimum(asked_tile, tile_count - 1)
    used_rows = asked_used[:, None, None]
    reply_left = jnp.where(
        used_rows, jnp.take(own_left, asked_safe, axis=0), jnp.zeros((), own_left.dtype)
    )
    reply_right = jnp.where(
        used_rows, jnp.take(own_right, asked_safe, axis=0), jnp.zeros((), own_left.dtype)
    )
    reply_rank = jnp.where(asked_used, jnp.take(own_rank, asked_safe), 0)
    reply_target = jnp.where(asked_used, jnp.take(own_target, asked_safe), 0)
    reply_shape = (peer_count, CAP)
    received = (
        *in_one_piece(
            (
                reply_left.reshape(reply_shape + own_left.shape[1:]),
                reply_right.reshape(reply_shape + own_left.shape[1:]),
            ),
            "col",
            0,
            0,
            1,
        ),
        *in_one_piece(
            (reply_rank.reshape(reply_shape), reply_target.reshape(reply_shape)), "col", 0, 0, 1
        ),
    )
    mine_left = jnp.take(flatten_peers(received[0]), buffer_place, axis=0)
    mine_right = jnp.take(flatten_peers(received[1]), buffer_place, axis=0)
    mine_rank = jnp.take(flatten_peers(received[2]), buffer_place)
    mine_target = jnp.take(flatten_peers(received[3]), buffer_place)
    new_left, returned_right = jax.vmap(recompress)(
        mine_left,
        mine_right,
        mine_rank,
        update_left[0],
        update_right[0],
        update_rank[0],
        mine_target,
    )
    send_left = pack_rows(new_left, filled, source_slot, peer_count)
    came_back = flatten_peers(exchange_in_pieces(send_left, "col", 2, 0, 0))
    tile_hit, arrival_index = match_tiles(asked_tile, tile_count)
    kept_left = jnp.where(
        tile_hit[:, None, None], jnp.take(came_back, arrival_index, axis=0), masked_left
    )
    squares = jnp.sum(jnp.square(kept_left.astype(jnp.float32)), axis=2)
    partial_rows = jnp.sum(squares.reshape(tile_count // BR, BR, squares.shape[1]), axis=0)
    row_sum = taken_together(partial_rows, "col")
    front_sum = taken_together(jnp.sum(row_sum), "row")
    mean_value = front_sum / (lax.axis_size("row") * BR * row_sum.shape[1])
    row_scale = jnp.sqrt(row_sum / mean_value)
    return (kept_left[None], returned_right[None], row_scale)


def solution(mesh):
    return jax.shard_map(
        local,
        mesh=mesh,
        in_specs=(
            P("row", "col", None, None),
            P("row", "col", None, None),
            P("row", "col"),
            P("row", "col"),
            P("row", "col", None, None),
            P("row", "col", None, None),
            P("row", "col"),
            P("row", "col"),
        ),
        out_specs=(P("row", "col", None, None), P("row", "col", None, None), P("row", None)),
        check_vma=False,
    )
```

profile of v0, /device:TPU:1, one launch (start us, length us, event | category | flops | bytes accessed | tf_op | source)
XLA Modules:
  0.0 450.7 jit_solution(8686211469081733182)
XLA Ops:
  4.3 14.7 %all_to_all.44 = s32[16,1,2]{2,1,0:T(1,128)S(1)} all-to-all(s32[16,1,2]{2,1,0:T(1,128)S(1)} %bitcast.119), channel_id=1, replica_groups=mesh['row'=8,'col'=16] {'col'}, dimensions={0} | all-to-all | bytes 256 | tf_op jit(solution)/shard_map/all_to_all | solution.py:178
  20.3 5.9 %gather_fusion.3 = bf16[32,768,128]{2,1,0:T(8,128)(2,1)} fusion(bf16[16,768,128]{2,1,0:T(8,128)(2,1)} %bitcast.112, s32[1024]{0:T(1024)S(1)} %pad_clamp_fusion.2), kind=kCustom, calls=%fused_computation.clone | custom fusion | bytes 12583040 | tf_op jit(solution)/shard_map/jit(_take)/gather | solution.py:184
  26.2 4.0 gather_fusion.4
  32.7 3.5 all-to-all-start.2
  36.1 5.7 %select_select_fusion.1 = (bf16[32,768,128]{2,1,0:T(8,128)(2,1)S(1)}, bf16[32,768,128]{2,1,0:T(8,128)(2,1)S(1)}) fusion(bf16[32,768,128]{2,1,0:T(8,128)(2,1)} %gather_fusion.3, pred[32]{0:T(512)(128)(4,1)S(1)} %get-tuple-element.28, pred[32]{0:T(512)(128)(4,1)S(1)} %get-tuple-element.27, bf16[32,768,128]{2,1,0:T(8,128)(2,1)} %gather_fusion.4), kind=kLoop, calls=%fused_computation.14 | loop fusion | flops 12582912 | bytes 25165888 | tf_op jit(solution)/shard_map/jit(_where)/select_n | solution.py:183
  41.9 5.3 %pad_maximum_fusion = bf16[16,4,768,128]{3,2,1,0:T(8,128)(2,1)} fusion(bf16[16,2,768,128]{3,2,1,0:T(8,128)(2,1)S(1)} %bitcast.115, bf16[16,2,768,128]{3,2,1,0:T(8,128)(2,1)S(1)} %bitcast.114), kind=kLoop, calls=%fused_computation.11 | loop fusion | flops 6291456 | bytes 25165824 | tf_op jit(solution)/shard_map/concatenate | solution.py:15
  47.2 6.8 %all-to-all-start.1 = ((bf16[16,4,768,128]{3,2,1,0:T(8,128)(2,1)}), bf16[16,4,768,128]{3,2,1,0:T(8,128)(2,1)}, u32[]{:S(2)}, u32[]{:S(2)}) async-start(bf16[16,4,768,128]{3,2,1,0:T(8,128)(2,1)} %pad_maximum_fusion), calls=%async_computation.1 | async-start | bytes 25165824 | tf_op jit(solution)/shard_map/all_to_all | solution.py:17
  56.2 178.3 %all-to-all-done.1 = bf16[16,4,768,128]{3,2,1,0:T(8,128)(2,1)} async-done(((bf16[16,4,768,128]{3,2,1,0:T(8,128)(2,1)}), bf16[16,4,768,128]{3,2,1,0:T(8,128)(2,1)}, u32[]{:S(2)}, u32[]{:S(2)}) %all-to-all-start.1) | async-done | bytes 12582944 | tf_op jit(solution)/shard_map/all_to_all | solution.py:17
  234.5 12.3 %fusion.82 = (bf16[16,2,768,128]{3,2,1,0:T(8,128)(2,1)}, bf16[16,2,768,128]{3,2,1,0:T(8,128)(2,1)}) fusion(bf16[16,4,768,128]{3,2,1,0:T(8,128)(2,1)} %all-to-all-done.1), kind=kLoop, calls=%fused_computation.172 | loop fusion | bytes 25165824 | tf_op jit(solution)/shard_map/slice | solution.py:22
  246.8 3.6 gather_fusion.5
  250.5 3.6 gather_fusion.9
  255.8 1.8 multiply_reduce_fusion.1
  257.6 1.5 fusion.51
  260.3 2.5 fusion.3
  262.9 2.2 fusion.85
  265.1 2.8 fusion.8
  267.9 2.3 fusion.9
  270.2 2.2 fusion.86
  272.4 2.3 fusion.11
  274.7 2.2 fusion.55
  276.9 2.2 fusion.16
  279.1 2.3 fusion.14
  281.7 2.0 fusion.80
  283.7 1.4 fusion.27
  285.0 1.9 fusion.87
  288.1 2.1 fusion.88
  291.4 1.9 fusion.89
  294.5 1.9 fusion.90
  297.6 2.0 fusion.91
  300.8 2.3 fusion.92
  304.3 1.9 fusion.93
  308.4 2.1 fusion.12
  312.5 4.0 gather_fusion.1
  316.5 3.5 select_select_fusion.2
  320.0 2.1 fusion.83
  322.1 41.5 %all_to_all.45 = bf16[16,1,2,384,128]{4,3,2,1,0:T(8,128)(2,1)} all-to-all(bf16[16,1,2,384,128]{4,3,2,1,0:T(8,128)(2,1)S(1)} %get-tuple-element.13), channel_id=1, replica_groups=mesh['row'=8,'col'=16] {'col'}, dimensions={0} | all-to-all | bytes 6291456 | tf_op jit(solution)/shard_map/all_to_all | solution.py:49
  363.6 4.8 %all-to-all-start.4 = ((bf16[16,1,2,384,128]{4,3,2,1,0:T(8,128)(2,1)}), bf16[16,1,2,384,128]{4,3,2,1,0:T(8,128)(2,1)}, u32[]{:S(2)}, u32[]{:S(2)}) async-start(bf16[16,1,2,384,128]{4,3,2,1,0:T(8,128)(2,1)} %get-tuple-element.14), calls=%async_computation.4 | async-start | bytes 6291456 | tf_op jit(solution)/shard_map/all_to_all | solution.py:49
  368.7 4.0 fusion.10
  372.8 2.1 fusion.5
  375.9 2.2 fusion.18
  378.1 26.4 %all-to-all-done.4 = bf16[16,1,2,384,128]{4,3,2,1,0:T(8,128)(2,1)} async-done(((bf16[16,1,2,384,128]{4,3,2,1,0:T(8,128)(2,1)}), bf16[16,1,2,384,128]{4,3,2,1,0:T(8,128)(2,1)}, u32[]{:S(2)}, u32[]{:S(2)}) %all-to-all-start.4) | async-done | bytes 3145760 | tf_op jit(solution)/shard_map/all_to_all | solution.py:49
  404.5 5.2 %pad_maximum_fusion.1 = bf16[16,1,2,768,128]{4,3,2,1,0:T(8,128)(2,1)} fusion(bf16[16,1,2,384,128]{4,3,2,1,0:T(8,128)(2,1)} %all-to-all-done.4, bf16[16,1,2,384,128]{4,3,2,1,0:T(8,128)(2,1)S(1)} %copy-done.8), kind=kLoop, calls=%fused_computation.12 | loop fusion | flops 12582912 | bytes 12582912 | tf_op jit(solution)/shard_map/concatenate | solution.py:50
  409.8 5.5 %gather_fusion.2 = bf16[16,768,128]{2,1,0:T(8,128)(2,1)} fusion(bf16[32,768,128]{2,1,0:T(8,128)(2,1)} %bitcast.116, s32[1024]{0:T(1024)S(1)} %pad_clamp_fusion), kind=kCustom, calls=%fused_computation.10 | custom fusion | bytes 6291520 | tf_op jit(solution)/shard_map/jit(_take)/gather | solution.py:224
  415.3 3.6 multiply_reduce_fusion
  419.7 9.4 %all-to-all-start.5 = ((f32[16,2,768]{2,1,0:T(2,128)}), f32[16,2,768]{2,1,0:T(2,128)S(1)}, u32[]{:S(2)}, u32[]{:S(2)}) async-start(f32[16,2,768]{2,1,0:T(2,128)} %broadcast_in_dim.235), calls=%async_computation.5 | async-start | bytes 196608 | tf_op jit(solution)/shard_map/all_to_all | solution.py:55
  429.1 5.2 %fusion = bf16[1,16,768,128]{3,2,1,0:T(8,128)(2,1)} fusion(bf16[16,768,128]{2,1,0:T(8,128)(2,1)} %gather_fusion.2, bf16[1,16,768,128]{3,2,1,0:T(8,128)(2,1)} %param.16, pred[16]{0:T(512)(128)(4,1)S(1)} %compare_and_fusion.3, pred[16]{0:T(512)(128)(4,1)S(1)} %fusion.58, pred[16,128]{1,0:T(8,128)(4,1)S(1)} %iota_compare_fusion.3), kind=kLoop, calls=%fused_computation.20 | loop fusion | flops 4718592 | bytes 9439264 | tf_op jit(solution)/shard_map/jit(_where)/select_n | solution.py:223
  434.3 1.5 all-to-all-done.5
  437.1 11.5 %all_to_all.46 = f32[8,1,1]{2,1,0:T(1,128)S(1)} all-to-all(f32[8,1,1]{2,1,0:T(1,128)S(1)} %broadcast_in_dim.236), channel_id=1, replica_groups=mesh['row'=8,'col'=16] {'row'}, dimensions={0} | all-to-all | bytes 64 | tf_op jit(solution)/shard_map/all_to_all | solution.py:55
  (112 shorter events, 28.6 us)
Async XLA Ops:
  0.6 25.5 %copy-start = (bf16[1,16,768,128]{3,2,1,0:T(8,128)(2,1)S(1)}, bf16[1,16,768,128]{3,2,1,0:T(8,128)(2,1)}, u32[]{:S(2)}) copy-start(bf16[1,16,768,128]{3,2,1,0:T(8,128)(2,1)} %param.17) | copy-start | bytes 9437188
  26.2 4.0 copy-start.2
  26.2 4.7 %copy-start.3 = (s32[1,16]{1,0:T(1,128)S(1)}, s32[1,16]{1,0:T(1,128)}, u32[]{:S(2)}) copy-start(s32[1,16]{1,0:T(1,128)} %param.19) | copy-start | bytes 196
  32.7 14.5 %all-to-all-start.2 = ((s32[16,1,4]{2,1,0:T(1,128)}), s32[16,1,4]{2,1,0:T(1,128)S(1)}, u32[]{:S(2)}, u32[]{:S(2)}) async-start(s32[16,1,4]{2,1,0:T(1,128)} %copy.77), calls=%async_computation.2 | async-start | bytes 16384 | tf_op jit(solution)/shard_map/all_to_all | solution.py:17
  47.2 8.9 %copy-start.13 = (s32[1,8]{1,0:T(1,128)S(1)}, s32[1,8]{1,0:T(1,128)}, u32[]{:S(2)}) copy-start(s32[1,8]{1,0:T(1,128)} %param.22) | copy-start | bytes 100
  47.2 187.3 %all-to-all-start.1 = ((bf16[16,4,768,128]{3,2,1,0:T(8,128)(2,1)}), bf16[16,4,768,128]{3,2,1,0:T(8,128)(2,1)}, u32[]{:S(2)}, u32[]{:S(2)}) async-start(bf16[16,4,768,128]{3,2,1,0:T(8,128)(2,1)} %pad_maximum_fusion), calls=%async_computation.1 | async-start | bytes 25165824 | tf_op jit(solution)/shard_map/all_to_all | solution.py:17
  254.1 1.6 copy-start.15
  254.5 3.1 copy-start.11
  267.9 2.3 copy-start.5
  272.4 2.3 copy-start.7
  272.4 2.3 copy-start.14
  307.4 1.0 copy-start.9
  363.6 5.1 %copy-start.6 = (f32[8,256,256]{2,1,0:T(8,128)S(1)}, f32[8,256,256]{2,1,0:T(8,128)}, u32[]{:S(2)}) copy-start(f32[8,256,256]{2,1,0:T(8,128)} %copy-done.5) | copy-start | bytes 6291460
  363.6 40.9 %all-to-all-start.4 = ((bf16[16,1,2,384,128]{4,3,2,1,0:T(8,128)(2,1)}), bf16[16,1,2,384,128]{4,3,2,1,0:T(8,128)(2,1)}, u32[]{:S(2)}, u32[]{:S(2)}) async-start(bf16[16,1,2,384,128]{4,3,2,1,0:T(8,128)(2,1)} %get-tuple-element.14), calls=%async_computation.4 | async-start | bytes 6291456 | tf_op jit(solution)/shard_map/all_to_all | solution.py:49
  368.7 4.0 copy-start.10
  372.7 2.1 copy-start.12
  372.7 2.1 copy-start.16
  375.9 28.7 %copy-start.8 = (bf16[16,1,2,384,128]{4,3,2,1,0:T(8,128)(2,1)S(1)}, bf16[16,1,2,384,128]{4,3,2,1,0:T(8,128)(2,1)}, u32[]{:S(2)}) copy-start(bf16[16,1,2,384,128]{4,3,2,1,0:T(8,128)(2,1)} %all_to_all.45) | copy-start | bytes 9437188
  409.8 5.6 %copy-start.4 = (bf16[1,16,768,128]{3,2,1,0:T(8,128)(2,1)S(1)}, bf16[1,16,768,128]{3,2,1,0:T(8,128)(2,1)}, u32[]{:S(2)}) copy-start(bf16[1,16,768,128]{3,2,1,0:T(8,128)(2,1)} %param.16) | copy-start | bytes 9437188
  419.7 16.1 %all-to-all-start.5 = ((f32[16,2,768]{2,1,0:T(2,128)}), f32[16,2,768]{2,1,0:T(2,128)S(1)}, u32[]{:S(2)}, u32[]{:S(2)}) async-start(f32[16,2,768]{2,1,0:T(2,128)} %broadcast_in_dim.235), calls=%async_computation.5 | async-start | bytes 196608 | tf_op jit(solution)/shard_map/all_to_all | solution.py:55
  429.1 21.4 %copy-start.1 = (bf16[1,16,768,128]{3,2,1,0:T(8,128)(2,1)S(1)}, bf16[1,16,768,128]{3,2,1,0:T(8,128)(2,1)}, u32[]{:S(2)}) copy-start(bf16[1,16,768,128]{3,2,1,0:T(8,128)(2,1)} %param.17) | copy-start | bytes 9437188
where the time goes:
time: 456 us; the launch traced here: 451 us
  waiting for transfers between devices  206 us (45%)
  blocking collectives  67.7 us (15%)
  matrix products  64.5 us (14%)
  local copies, waits for them, and re-layouts  50.7 us (11%)
  other arithmetic  35.1 us (8%)
  starting transfers between devices  24.4 us (5%)
    all_to_all x2, waiting for transfers between devices, in_one_piece(): lax.all_to_all(both, axis, split_axis=split_dim, concat_axis=concat_dim,...  178 us
    dot_general x29, matrix products, high_dot(): return jnp.dot(first, second, precision=lax.Precision.HIGHEST)  55.3 us
    all_to_all x1, blocking collectives, exchange_in_pieces(): lax.all_to_all(slab, axis, split_axis=0, concat_axis=0, tiled=True)  41.5 us
    all_to_all x1, waiting for transfers between devices, exchange_in_pieces(): lax.all_to_all(slab, axis, split_axis=0, concat_axis=0, tiled=True)  26.4 us
    all_to_all x1, blocking collectives, local(): lax.all_to_all(tile_buffer, 'col', split_axis=0, concat_axis=0, tiled=True)  14.7 us
    slice x4, local copies, waits for them, and re-layouts, in_one_piece(): done.append(lax.slice_in_dim(filled, at, at + a.shape[along], axis=along))  12.5 us
    all_to_all x1, blocking collectives, copy_for_each(): return lax.all_to_all(copies, axis, split_axis=0, concat_axis=0, tiled=True)  11.5 us
    all_to_all x2, starting transfers between devices, in_one_piece(): lax.all_to_all(both, axis, split_axis=split_dim, concat_axis=concat_dim,...  10.2 us
  transfers between devices with their start and end apart: 4, of which 3 were waited for; matrix products, arithmetic and copies ran while one was open for 6% of the time, Pallas kernels for 0%

commit v1 on v0

v1 whole, which is shorter than its diff:
```python
import math

import jax
import jax.numpy as jnp
from jax import lax
from jax.experimental import pallas as pl
from jax.experimental.pallas import tpu as pltpu
from jax.sharding import PartitionSpec as P

BR = 2
SWEEPS = 8
ROOTS = 3
TOGETHER = 2
HALFWAY = 4
F32 = jnp.float32
BF16 = jnp.bfloat16
TAIL = 16


def parts_of(value):
    high = value.astype(BF16)
    return high, (value - high.astype(F32)).astype(BF16)


def plain(first, second):
    return jnp.dot(first, second, preferred_element_type=F32)


def over_rows(first, second):
    return lax.dot_general(first, second, (((0,), (0,)), ((), ())), preferred_element_type=F32)


def wide(first, second):
    return plain(first[0], second[0]) + (plain(first[0], second[1]) + plain(first[1], second[0]))


def tall(first, second):
    half = second[0].shape[1]
    both = plain(first[0], jnp.concatenate(second, axis=1))
    return both[:, :half] + (both[:, half:] + plain(first[1], second[0]))


def narrow(first, second):
    half = second[0].shape[1]
    right = jnp.concatenate(second, axis=1)
    both = plain(jnp.concatenate(first, axis=1), jnp.concatenate([right, right], axis=0))
    return both[:, :half] + both[:, half:]


def self_product(value):
    both = jnp.concatenate(value, axis=1)
    half = value[0].shape[1]
    four = over_rows(both, both)
    return (four[:half, :half] + four[half:, half:]) + (four[:half, half:] + four[half:, :half])


def eye(order):
    return (
        lax.broadcasted_iota(jnp.int32, (order, order), 0)
        == lax.broadcasted_iota(jnp.int32, (order, order), 1)
    ).astype(F32)


def total_of(value):
    return jnp.sum(jnp.sum(value, axis=1, keepdims=True), axis=0, keepdims=True)


def recompress_body(meta, own, width, left_in, right_in, add_left, add_right, left_out, right_out):
    half = add_left.shape[2]
    rows = add_left.shape[1]
    piece = left_in.shape[1] // TOGETHER
    tiles_each = width[0]
    lane = lax.broadcasted_iota(jnp.int32, (1, half), 1)
    which = range(TOGETHER)
    ident = eye(2 * half)
    left, right, keep, gram_left, gram_right = [], [], [], [], []
    for n in which:
        spot = pl.program_id(0) * TOGETHER + n
        slot = own[0, spot]
        owner, place = slot // tiles_each, slot % tiles_each
        old_live = (lane < meta[owner, place]).astype(F32)
        add_live = (lane < own[1, spot]).astype(F32)
        keep.append((lane < meta[owner, tiles_each + place]).astype(F32))
        live = jnp.concatenate([old_live, add_live], axis=1)
        narrow_live = live.astype(BF16)

        def stacked(ref, add):
            old = ref[:, n * piece : (n + 1) * piece, :].reshape(rows, half)
            return jnp.concatenate([old, add[n]], axis=1) * narrow_live

        left.append(stacked(left_in, add_left))
        right.append(stacked(right_in, add_right))
        gram_right.append(over_rows(right[n], right[n]) + ident * (1.0 - live))
        gram_left.append(over_rows(left[n], left[n]))
    scale, root, inverse = [], [], []
    for n in which:
        scale.append(jnp.sqrt(total_of(gram_right[n] * gram_right[n])))
        root.append(gram_right[n] / scale[n])
    for n in which:
        middle = 1.5 * ident - 0.5 * root[n]
        cut = parts_of(middle)
        root[n] = wide(parts_of(root[n]), cut)
        inverse.append(middle)
    for repeat in range(1, ROOTS):
        for n in which:
            root_cut, inverse_cut = parts_of(root[n]), parts_of(inverse[n])
            middle = parts_of(1.5 * ident - 0.5 * wide(inverse_cut, root_cut))
            root[n] = wide(root_cut, middle)
            inverse[n] = wide(middle, inverse_cut)
    root = [parts_of(r) for r in root]
    inverse = [parts_of(r) for r in inverse]
    space = []
    for n in which:
        full = root[n][0].astype(F32) + root[n][1].astype(F32)
        folded = parts_of(full[:, :half] + full[:, half:])
        core = tall(root[n], parts_of(tall(parts_of(gram_left[n]), folded))) * scale[n]
        space.append(core / jnp.sqrt(total_of(core * core) + 1e-06))
    ident = eye(half)
    for block in range(SWEEPS // HALFWAY):
        cut = [parts_of(space[n]) for n in which]
        inner = [self_product(cut[n]) for n in which]
        gathered = [None] * TOGETHER
        for repeat in range(HALFWAY):
            for n in which:
                factor = parts_of(1.5 * ident - 0.5 * inner[n])
                if repeat + 1 < HALFWAY:
                    inner[n] = narrow(parts_of(narrow(parts_of(inner[n]), factor)), factor)
                gathered[n] = factor if repeat == 0 else parts_of(narrow(gathered[n], factor))
        space = [narrow(cut[n], gathered[n]) for n in which]
    for n in which:
        kept = parts_of(space[n] * keep[n])
        square_root = jnp.sqrt(scale[n])
        on_left = jnp.concatenate(parts_of(tall(root[n], kept) * square_root), axis=1)
        on_right = jnp.concatenate(parts_of(tall(inverse[n], kept) / square_root), axis=1)
        new_left = plain(left[n], on_left)
        new_left = (new_left[:, :half] + new_left[:, half:]).astype(BF16)
        left_out[:, n * piece : (n + 1) * piece, :] = new_left.reshape(-1, piece, half)
        new_right = plain(right[n], on_right)
        new_right = (new_right[:, :half] + new_right[:, half:]) * math.sqrt(rows)
        right_out[n] = new_right.astype(BF16)


def recompress(meta, own, width, arrived, add_left, add_right):
    peers, span, half = arrived.shape
    slots, rows, _ = add_left.shape
    piece = rows // peers
    steps = slots // TOGETHER
    pieces = (peers, TOGETHER * piece, half)
    whole = (TOGETHER, rows, half)
    return pl.pallas_call(
        recompress_body,
        grid_spec=pltpu.PrefetchScalarGridSpec(
            num_scalar_prefetch=3,
            grid=(steps,),
            in_specs=[
                pl.BlockSpec(pieces, lambda g, *_: (0, g, 0)),
                pl.BlockSpec(pieces, lambda g, *_: (0, g + steps, 0)),
                pl.BlockSpec(whole, lambda g, *_: (g, 0, 0)),
                pl.BlockSpec(whole, lambda g, *_: (g, 0, 0)),
            ],
            out_specs=[
                pl.BlockSpec(pieces, lambda g, *_: (0, g, 0)),
                pl.BlockSpec(whole, lambda g, *_: (g, 0, 0)),
            ],
        ),
        out_shape=[
            jax.ShapeDtypeStruct((peers, slots * piece, half), BF16),
            jax.ShapeDtypeStruct((slots, rows, half), BF16),
        ],
        compiler_params=pltpu.CompilerParams(
            dimension_semantics=("arbitrary",), vmem_limit_bytes=60 * 2**20
        ),
        name="recompress",
    )(meta, own, width, arrived, arrived, add_left, add_right)


def pack_body(left, right, meta, out, done):
    tiles, rows, _ = left.shape
    peers = out.shape[0]
    piece = rows // peers

    def one_peer(peer, carry):
        def one_tile(tile, inner):
            source = pl.ds(pl.multiple_of(peer * piece, TAIL), piece)
            for at, ref in ((0, left), (tiles * piece, right)):
                target = pl.ds(pl.multiple_of(at + tile * piece, TAIL), piece)
                pltpu.make_async_copy(ref.at[tile, source], out.at[peer, target], done).start()
            return inner

        lax.fori_loop(0, tiles, one_tile, 0, unroll=4)
        pltpu.make_async_copy(meta, out.at[peer, pl.ds(2 * tiles * piece, TAIL)], done).start()
        return carry

    lax.fori_loop(0, peers, one_peer, 0)
    pltpu.make_async_copy(out, out, done).wait()


def in_memory():
    return pl.BlockSpec(memory_space=pltpu.HBM)


def pack(left, right, meta, peers):
    tiles, rows, half = left.shape
    span = 2 * tiles * (rows // peers) + TAIL
    return pl.pallas_call(
        pack_body,
        in_specs=[in_memory()] * 3,
        out_specs=in_memory(),
        out_shape=jax.ShapeDtypeStruct((peers, span, half), BF16),
        scratch_shapes=[pltpu.SemaphoreType.DMA],
        name="pack",
    )(left, right, meta)


def pick_body(tiles, meta, pieces, out, named_by, done):
    peers, span, _ = pieces.shape
    piece = (span - TAIL) // (2 * tiles)
    slots = out.shape[1] // (2 * piece)

    def one_peer(peer, carry):
        for s in range(slots):
            slot = meta[peer, 2 * tiles + s]
            owner, place = slot // tiles, slot % tiles
            for at, to in ((0, 0), (tiles * piece, slots * piece)):
                source = pl.ds(pl.multiple_of(at + place * piece, TAIL), piece)
                pltpu.make_async_copy(
                    pieces.at[owner, source], out.at[peer, pl.ds(to + s * piece, piece)], done
                ).start()
        return carry

    lax.fori_loop(0, peers, one_peer, 0)

    def clear(tile, carry):
        named_by[tile] = -1
        return carry

    lax.fori_loop(0, peers * tiles, clear, 0, unroll=8)

    def note(peer, carry):
        for s in range(slots):
            named_by[meta[peer, 2 * tiles + s]] = peer * slots + s
        return carry

    lax.fori_loop(0, peers, note, 0)
    pltpu.make_async_copy(out, out, done).wait()


def pick(meta, pieces, tiles, slots):
    peers, span, half = pieces.shape
    piece = (span - TAIL) // (2 * tiles)

    def body(*refs):
        pick_body(tiles, *refs)

    return pl.pallas_call(
        body,
        in_specs=[pl.BlockSpec(memory_space=pltpu.SMEM), in_memory()],
        out_specs=[in_memory(), pl.BlockSpec(memory_space=pltpu.SMEM)],
        out_shape=[
            jax.ShapeDtypeStruct((peers, 2 * slots * piece, half), BF16),
            jax.ShapeDtypeStruct((peers * tiles,), jnp.int32),
        ],
        scratch_shapes=[pltpu.SemaphoreType.DMA],
        name="pick",
    )(meta, pieces)


def place_body(tiles, meta, named_by, fresh, old, out, sums):
    peers, span, half = fresh.shape
    piece = old.shape[1] // tiles
    slots = span // piece
    lane = lax.broadcasted_iota(jnp.int32, (piece, half), 1)

    def one_owner(owner, totals):
        totals = list(totals)
        for tile in range(tiles):
            who = named_by[owner * tiles + tile]
            safe = jnp.maximum(who, 0)
            at = pl.multiple_of((safe % slots) * piece, TAIL)
            new = fresh[safe // slots, pl.ds(at, piece), :].astype(F32)
            own = old[owner, tile * piece : (tile + 1) * piece, :].astype(F32)
            limit = jnp.where(who < 0, meta[owner, tile], half)
            value = jnp.where(lane < limit, jnp.where(who < 0, own, new), 0.0)
            out[owner, tile * piece : (tile + 1) * piece, :] = value.astype(BF16)
            totals[tile % BR] += value * value
        return tuple(totals)

    totals = lax.fori_loop(
        0, peers, one_owner, tuple(jnp.zeros((piece, half), F32) for _ in range(BR))
    )
    tail_lane = lax.broadcasted_iota(jnp.int32, (TAIL, half), 1)
    tail = jnp.zeros((TAIL, half), F32)
    whole = jnp.zeros((1, 1), F32)
    for k in range(BR):
        row = jnp.sum(totals[k], axis=1, keepdims=True)
        whole += jnp.sum(row, axis=0, keepdims=True)
        for group in range(piece // TAIL):
            rest = row[group * TAIL : (group + 1) * TAIL]
            for part in range(3):
                high = rest.astype(BF16).astype(F32)
                rest = rest - high
                tail = jnp.where(tail_lane == (group * BR + k) * 3 + part, high, tail)
    tail = tail.astype(BF16)
    for peer in range(peers):
        out[peer, tiles * piece :, :] = tail
    sums[...] = jnp.broadcast_to(whole, sums.shape)


def place(meta, named_by, fresh, pieces, tiles):
    peers, span, half = fresh.shape
    piece = (pieces.shape[1] - TAIL) // (2 * tiles)

    def body(*refs):
        place_body(tiles, *refs)

    return pl.pallas_call(
        body,
        grid=(1,),
        in_specs=[
            pl.BlockSpec(memory_space=pltpu.SMEM),
            pl.BlockSpec(memory_space=pltpu.SMEM),
            pl.BlockSpec(fresh.shape, lambda g: (0, 0, 0)),
            pl.BlockSpec((peers, tiles * piece, half), lambda g: (0, 0, 0)),
        ],
        out_specs=[
            pl.BlockSpec((peers, tiles * piece + TAIL, half), lambda g: (0, 0, 0)),
            pl.BlockSpec((8, half), lambda g: (0, 0)),
        ],
        out_shape=[
            jax.ShapeDtypeStruct((peers, tiles * piece + TAIL, half), BF16),
            jax.ShapeDtypeStruct((8, half), F32),
        ],
        compiler_params=pltpu.CompilerParams(vmem_limit_bytes=60 * 2**20),
        name="place",
    )(meta, named_by, fresh, pieces)


def exchange(value, axis):
    return lax.all_to_all(value, axis, split_axis=0, concat_axis=0, tiled=True)


def local(
    current_left,
    current_right,
    current_rank,
    target_rank,
    update_left,
    update_right,
    update_rank,
    owner_slot,
):
    peers = lax.axis_size("col")
    tiles, rows, half = current_left.shape[1:]
    slots = owner_slot.shape[1]
    piece = rows // peers
    table = jnp.concatenate([current_rank, target_rank, owner_slot], axis=1).astype(BF16)
    table = jnp.pad(table, ((0, TAIL - 1), (0, half - table.shape[1])))
    pieces = exchange(pack(current_left[0], current_right[0], table, peers), "col")
    meta = pieces[:, 2 * tiles * piece, :].astype(jnp.int32)
    own = jnp.concatenate([owner_slot, update_rank], axis=0)
    width = jnp.full((1,), tiles, jnp.int32)
    chosen, named_by = pick(meta, pieces, tiles, slots)
    arrived = exchange(chosen, "col")
    fresh, returned_right = recompress(meta, own, width, arrived, update_left[0], update_right[0])
    fresh = exchange(fresh, "col")
    placed, sums = place(meta, named_by, fresh, pieces, tiles)
    placed = exchange(placed, "col")
    kept_left = placed[:, : tiles * piece].reshape(peers, tiles, piece, half)
    kept_left = jnp.swapaxes(kept_left, 0, 1).reshape(tiles, rows, half)
    groups = piece // TAIL
    tail = placed[:, tiles * piece :, : groups * BR * 3].astype(F32)
    tail = jnp.sum(tail.reshape(peers, TAIL, groups, BR, 3), axis=4)
    row_sum = jnp.transpose(tail, (3, 0, 2, 1)).reshape(BR, rows)
    row_total = jnp.broadcast_to(jnp.sum(row_sum), (lax.axis_size("row"), 1, 1))
    front_sum = jnp.sum(exchange(row_total, "row"))
    mean_value = front_sum / (lax.axis_size("row") * BR * rows)
    row_scale = jnp.sqrt(row_sum / mean_value)
    return (kept_left[None], returned_right[None], row_scale)


def solution(mesh):
    return jax.shard_map(
        local,
        mesh=mesh,
        in_specs=(
            P("row", "col", None, None),
            P("row", "col", None, None),
            P("row", "col"),
            P("row", "col"),
            P("row", "col", None, None),
            P("row", "col", None, None),
            P("row", "col"),
            P("row", "col"),
        ),
        out_specs=(P("row", "col", None, None), P("row", "col", None, None), P("row", None)),
        check_vma=False,
    )
```

time: 456 us -> 552 us (1.21)
  Pallas kernels: 0 us -> 332 us
  waiting for transfers between devices: 206 us -> 44.6 us
  blocking collectives: 67.7 us -> 146 us
  matrix products: 64.5 us -> 0 us
  local copies, waits for them, and re-layouts: 50.7 us -> 9.3 us
  other arithmetic: 35.1 us -> 5.12 us
  starting transfers between devices: 24.4 us -> 13.1 us
    pallas_call x0 -> x4, Pallas kernels: none -> 332 us  [the longest x1 194 us: pack(): pl.pallas_call(pack_body, in_specs=[in_memory()] * 3, out_specs=in_memory...]
    all_to_all x4 -> x2, waiting for transfers between devices: 206 us -> 44.6 us  [exchange(): return lax.all_to_all(value, axis, split_axis=0, concat_axis=0, tiled=True)]
    all_to_all x3, blocking collectives: 67.7 us -> 146 us  [exchange(): return lax.all_to_all(value, axis, split_axis=0, concat_axis=0, tiled=True)]
    dot_general x35 -> x0, matrix products: 64.5 us -> none  [the longest x29 55.3 us: high_dot(): return jnp.dot(first, second, precision=lax.Precision.HIGHEST)]
    gather x12 -> x0, local copies, waits for them, and re-layouts: 30.2 us -> none  [the longest x1 5.91 us: local(): jnp.take(own_left, asked_safe, axis=0)]
    select_n x11 -> x0, other arithmetic: 15.6 us -> none  [the longest x1 5.71 us: local(): jnp.where(used_rows, jnp.take(own_left, asked_safe, axis=0), jnp.zeros(()...]
    slice x4 -> x1, local copies, waits for them, and re-layouts: 12.5 us -> 0.29 us  [local(): kept_left = placed[:, :tiles * piece].reshape(peers, tiles, piece, half)]
    all_to_all x4 -> x2, starting transfers between devices: 24.4 us -> 13.1 us  [exchange(): return lax.all_to_all(value, axis, split_axis=0, concat_axis=0, tiled=True)]
  transfers between devices with their start and end apart: 4 -> 2, of which waited for: 3 -> 2; matrix products, arithmetic and copies ran while one was open for 6% -> 1% of each run, Pallas kernels for 0% -> 0%
where the time goes in v1:
time: 552 us
  Pallas kernels  332 us (60%)
  blocking collectives  146 us (26%)
  waiting for transfers between devices  44.6 us (8%)
  starting transfers between devices  13.1 us (2%)
  local copies, waits for them, and re-layouts  9.3 us (2%)
    pallas_call x1, Pallas kernels, pack(): pl.pallas_call(pack_body, in_specs=[in_memory()] * 3, out_specs=in_memory...  194 us
    all_to_all x3, blocking collectives, exchange(): return lax.all_to_all(value, axis, split_axis=0, concat_axis=0, tiled=True)  146 us
    pallas_call x1, Pallas kernels, pick(): pl.pallas_call(body, in_specs=[pl.BlockSpec(memory_space=pltpu.SMEM), in_...  97.9 us
    all_to_all x2, waiting for transfers between devices, exchange(): return lax.all_to_all(value, axis, split_axis=0, concat_axis=0, tiled=True)  44.6 us
    pallas_call x1, Pallas kernels, recompress(): pl.pallas_call(recompress_body, grid_spec=pltpu.PrefetchScalarGridSpec(nu...  34.6 us
    all_to_all x2, starting transfers between devices, exchange(): return lax.all_to_all(value, axis, split_axis=0, concat_axis=0, tiled=True)  13.1 us
  transfers between devices with their start and end apart: 2, of which 2 were waited for; matrix products, arithmetic and copies ran while one was open for 1% of the time, Pallas kernels for 0%

profile of v1, /device:TPU:1, one launch (start us, length us, event | category | flops | bytes accessed | tf_op | source)
XLA Modules:
  0.0 551.7 jit_solution(3603651515024579207)
XLA Ops:
  0.6 0.7 convert.10
  1.3 0.7 convert.11
  1.9 0.7 convert.12
  2.6 0.7 fusion.9.meta
  3.3 193.9 %pack.1 = bf16[16,1552,128]{2,1,0:T(8,128)(2,1)} custom-call(bf16[16,768,128]{2,1,0:T(8,128)(2,1)} %bitcast.15, bf16[16,768,128]{2,1,0:T(8,128)(2,1)} %bitcast.16, bf16[16,128]{1,0:T(8,128)(2,1)} %fusion.9.meta), custom_call_target="tpu_custom_call" | custom-call | tf_op jit(solution)/shard_map/pack/pallas_call | solution.py:205
  197.2 81.5 %all_to_all.25.refs_1_.refs_3_ = bf16[16,1552,128]{2,1,0:T(8,128)(2,1)S(1)} all-to-all(bf16[16,1552,128]{2,1,0:T(8,128)(2,1)} %pack.1), channel_id=1, replica_groups=mesh['row'=8,'col'=16] {'col'}, dimensions={0} | all-to-all | bytes 12713984 | tf_op jit(solution)/shard_map/all_to_all | solution.py:339
  278.7 0.0 copy-start
  278.7 2.7 copy-done
  281.4 0.6 slice_convert_fusion.1
  282.0 97.9 %pick.1 = (bf16[16,768,128]{2,1,0:T(8,128)(2,1)}, s32[256]{0:T(256)}) custom-call(s32[16,128]{1,0:T(8,128)} %bitcast.20, bf16[16,1552,128]{2,1,0:T(8,128)(2,1)} %copy-done), custom_call_target="tpu_custom_call" | custom-call | tf_op jit(solution)/shard_map/pick/pallas_call | solution.py:255
  379.9 0.0 copy-start.2
  379.9 0.0 copy-start.3
  379.9 3.8 all-to-all-start.1
  383.7 0.0 copy-done.2
  383.7 0.0 copy-done.3
  383.7 0.6 pad_add_fusion.own
  384.3 43.1 %all-to-all-done.1.left_in.right_in = bf16[16,768,128]{2,1,0:T(8,128)(2,1)S(1)} async-done(((bf16[16,768,128]{2,1,0:T(8,128)(2,1)}), bf16[16,768,128]{2,1,0:T(8,128)(2,1)S(1)}, u32[]{:S(2)}, u32[]{:S(2)}) %all-to-all-start.1) | async-done | bytes 3145760 | tf_op jit(solution)/shard_map/all_to_all | solution.py:339
  427.3 0.0 copy-start.1
  427.3 1.7 copy-done.1
  429.0 34.6 %recompress.1 = (bf16[16,384,128]{2,1,0:T(8,128)(2,1)}, bf16[8,768,128]{2,1,0:T(8,128)(2,1)}) custom-call(s32[16,128]{1,0:T(8,128)} %bitcast.21, s32[2,8]{1,0:T(2,128)} %pad_add_fusion.own, s32[1]{0:T(128)} %constant.3.clone.1.width, bf16[16,768,128]{2,1,0:T(8,128)(2,1)} %copy-done.1, bf16[16,768,128]{2,1,0:T(8,128)(2,1)} %copy-done.1, ...), custom_call_target="tpu_custom_call" | custom-call | tf_op jit(solution)/shard_map/recompress/pallas_call | solution.py:150
  463.6 24.1 %all_to_all.26.refs_2_ = bf16[16,384,128]{2,1,0:T(8,128)(2,1)} all-to-all(bf16[16,384,128]{2,1,0:T(8,128)(2,1)} %get-tuple-element.10), channel_id=1, replica_groups=mesh['row'=8,'col'=16] {'col'}, dimensions={0} | all-to-all | bytes 3145728 | tf_op jit(solution)/shard_map/all_to_all | solution.py:339
  487.7 6.1 %place.1 = (bf16[16,784,128]{2,1,0:T(8,128)(2,1)}, f32[8,128]{1,0:T(8,128)}) custom-call(s32[16,128]{1,0:T(8,128)} %bitcast.22, s32[256]{0:T(256)} %get-tuple-element.8.refs_1_, bf16[16,384,128]{2,1,0:T(8,128)(2,1)} %all_to_all.26.refs_2_, bf16[16,1552,128]{2,1,0:T(8,128)(2,1)} %copy-done), custom_call_target="tpu_custom_call" | custom-call | tf_op jit(solution)/shard_map/place/pallas_call | solution.py:316
  493.8 40.1 %all_to_all.27 = bf16[16,784,128]{2,1,0:T(8,128)(2,1)S(1)} all-to-all(bf16[16,784,128]{2,1,0:T(8,128)(2,1)} %get-tuple-element.11), channel_id=1, replica_groups=mesh['row'=8,'col'=16] {'col'}, dimensions={0} | all-to-all | bytes 6422528 | tf_op jit(solution)/shard_map/all_to_all | solution.py:339
  533.9 0.6 fusion
  534.6 1.2 broadcast_in_dim.7
  535.8 9.4 %all-to-all-start.4 = ((f32[8,1,1]{2,1,0:T(1,128)}), f32[8,1,1]{2,1,0:T(1,128)S(1)}, u32[]{:S(2)}, u32[]{:S(2)}) async-start(f32[8,1,1]{2,1,0:T(1,128)} %broadcast_in_dim.7), calls=%async_computation.4 | async-start | bytes 8192 | tf_op jit(solution)/shard_map/all_to_all | solution.py:339
  545.2 0.3 slice.13
  545.5 2.5 copy.20
  548.0 0.2 copy.21
  548.2 1.5 all-to-all-done.4
  549.7 0.6 reduce_sum.29
  551.0 0.7 sqrt.11
  (4 shorter events, 0.1 us)
Async XLA Ops:
  278.7 2.7 copy-start
  379.9 3.8 copy-start.2
  379.9 3.8 copy-start.3
  379.9 47.4 %all-to-all-start.1 = ((bf16[16,768,128]{2,1,0:T(8,128)(2,1)}), bf16[16,768,128]{2,1,0:T(8,128)(2,1)S(1)}, u32[]{:S(2)}, u32[]{:S(2)}) async-start(bf16[16,768,128]{2,1,0:T(8,128)(2,1)} %get-tuple-element.9), calls=%async_computation.1 | async-start | bytes 6291456 | tf_op jit(solution)/shard_map/all_to_all | solution.py:339
  427.3 1.7 copy-start.1
  535.8 13.9 %all-to-all-start.4 = ((f32[8,1,1]{2,1,0:T(1,128)}), f32[8,1,1]{2,1,0:T(1,128)S(1)}, u32[]{:S(2)}, u32[]{:S(2)}) async-start(f32[8,1,1]{2,1,0:T(1,128)} %broadcast_in_dim.7), calls=%async_computation.4 | async-start | bytes 8192 | tf_op jit(solution)/shard_map/all_to_all | solution.py:339

commit v2 on v1

--- a/solution.py
+++ b/solution.py
@@ -65,17 +65,17 @@
     return jnp.sum(jnp.sum(value, axis=1, keepdims=True), axis=0, keepdims=True)
 
 
-def recompress_body(meta, own, width, left_in, right_in, add_left, add_right, left_out, right_out):
-    half = add_left.shape[2]
-    rows = add_left.shape[1]
-    piece = left_in.shape[1] // TOGETHER
-    tiles_each = width[0]
+def recompress_step(step, meta, own, width, left_in, right_in, add_left, add_right, left_out, right_out):
+    _, rows, half = add_left.shape
+    peers = left_in.shape[0]
+    piece = rows // peers
+    tiles_each = width
     lane = lax.broadcasted_iota(jnp.int32, (1, half), 1)
     which = range(TOGETHER)
     ident = eye(2 * half)
     left, right, keep, gram_left, gram_right = [], [], [], [], []
     for n in which:
-        spot = pl.program_id(0) * TOGETHER + n
+        spot = step * TOGETHER + n
         slot = own[0, spot]
         owner, place = slot // tiles_each, slot % tiles_each
         old_live = (lane < meta[owner, place]).astype(F32)
@@ -84,12 +84,12 @@
         live = jnp.concatenate([old_live, add_live], axis=1)
         narrow_live = live.astype(BF16)
 
-        def stacked(ref, add):
-            old = ref[:, n * piece : (n + 1) * piece, :].reshape(rows, half)
-            return jnp.concatenate([old, add[n]], axis=1) * narrow_live
-
-        left.append(stacked(left_in, add_left))
-        right.append(stacked(right_in, add_right))
+        def stacked(ref, at, add):
+            old = ref[:, pl.ds(pl.multiple_of(at + spot * piece, TAIL), piece), :]
+            return jnp.concatenate([old.reshape(rows, half), add[spot]], axis=1) * narrow_live
+
+        left.append(stacked(left_in, 0, add_left))
+        right.append(stacked(right_in, right_in.shape[1] // 2, add_right))
         gram_right.append(over_rows(right[n], right[n]) + ident * (1.0 - live))
         gram_left.append(over_rows(left[n], left[n]))
     scale, root, inverse = [], [], []
@@ -134,140 +134,121 @@
         on_right = jnp.concatenate(parts_of(tall(inverse[n], kept) / square_root), axis=1)
         new_left = plain(left[n], on_left)
         new_left = (new_left[:, :half] + new_left[:, half:]).astype(BF16)
-        left_out[:, n * piece : (n + 1) * piece, :] = new_left.reshape(-1, piece, half)
+        spot = step * TOGETHER + n
+        left_out[:, pl.ds(pl.multiple_of(spot * piece, TAIL), piece), :] = new_left.reshape(
+            peers, piece, half
+        )
         new_right = plain(right[n], on_right)
         new_right = (new_right[:, :half] + new_right[:, half:]) * math.sqrt(rows)
-        right_out[n] = new_right.astype(BF16)
-
-
-def recompress(meta, own, width, arrived, add_left, add_right):
-    peers, span, half = arrived.shape
+        right_out[spot] = new_right.astype(BF16)
+
+
+def on_chip():
+    return pl.BlockSpec(memory_space=pltpu.VMEM)
+
+
+def scalars():
+    return pl.BlockSpec(memory_space=pltpu.SMEM)
+
+
+def recompress(meta, own, tiles, arrived, add_left, add_right):
+    peers, _, half = arrived.shape
     slots, rows, _ = add_left.shape
-    piece = rows // peers
-    steps = slots // TOGETHER
-    pieces = (peers, TOGETHER * piece, half)
-    whole = (TOGETHER, rows, half)
+
+    def body(meta, own, arrived, add_left, add_right, left_out, right_out):
+        def one_step(step, carry):
+            recompress_step(
+                step, meta, own, tiles, arrived, arrived, add_left, add_right, left_out, right_out
+            )
+            return carry
+
+        lax.fori_loop(0, slots // TOGETHER, one_step, 0)
+
     return pl.pallas_call(
-        recompress_body,
-        grid_spec=pltpu.PrefetchScalarGridSpec(
-            num_scalar_prefetch=3,
-            grid=(steps,),
-            in_specs=[
-                pl.BlockSpec(pieces, lambda g, *_: (0, g, 0)),
-                pl.BlockSpec(pieces, lambda g, *_: (0, g + steps, 0)),
-                pl.BlockSpec(whole, lambda g, *_: (g, 0, 0)),
-                pl.BlockSpec(whole, lambda g, *_: (g, 0, 0)),
-            ],
-            out_specs=[
-                pl.BlockSpec(pieces, lambda g, *_: (0, g, 0)),
-                pl.BlockSpec(whole, lambda g, *_: (g, 0, 0)),
-            ],
-        ),
+        body,
+        in_specs=[scalars(), scalars(), on_chip(), on_chip(), on_chip()],
+        out_specs=[on_chip(), on_chip()],
         out_shape=[
-            jax.ShapeDtypeStruct((peers, slots * piece, half), BF16),
+            jax.ShapeDtypeStruct((peers, slots * (rows // peers), half), BF16),
             jax.ShapeDtypeStruct((slots, rows, half), BF16),
         ],
-        compiler_params=pltpu.CompilerParams(
-            dimension_semantics=("arbitrary",), vmem_limit_bytes=60 * 2**20
-        ),
+        compiler_params=pltpu.CompilerParams(vmem_limit_bytes=60 * 2**20),
         name="recompress",
-    )(meta, own, width, arrived, arrived, add_left, add_right)
-
-
-def pack_body(left, right, meta, out, done):
-    tiles, rows, _ = left.shape
-    peers = out.shape[0]
+    )(meta, own, arrived, add_left, add_right)
+
+
+def pack(left, right, rank, target, slot, peers):
+    tiles, rows, half = left.shape
     piece = rows // peers
-
-    def one_peer(peer, carry):
-        def one_tile(tile, inner):
-            source = pl.ds(pl.multiple_of(peer * piece, TAIL), piece)
+    tail_at = 2 * tiles * piece
+
+    def body(left, right, rank, target, slot, out, table):
+        table[...] = jnp.zeros_like(table)
+        at = 0
+        for ref in (rank, target, slot):
+            wide_ref = ref.shape[1]
+            table[0:1, at : at + wide_ref] = ref[...]
+            at += wide_ref
+        tail = table[...].astype(F32).astype(BF16)
+
+        def one_tile(tile, carry):
             for at, ref in ((0, left), (tiles * piece, right)):
-                target = pl.ds(pl.multiple_of(at + tile * piece, TAIL), piece)
-                pltpu.make_async_copy(ref.at[tile, source], out.at[peer, target], done).start()
-            return inner
-
-        lax.fori_loop(0, tiles, one_tile, 0, unroll=4)
-        pltpu.make_async_copy(meta, out.at[peer, pl.ds(2 * tiles * piece, TAIL)], done).start()
-        return carry
-
-    lax.fori_loop(0, peers, one_peer, 0)
-    pltpu.make_async_copy(out, out, done).wait()
-
-
-def in_memory():
-    return pl.BlockSpec(memory_space=pltpu.HBM)
-
-
-def pack(left, right, meta, peers):
-    tiles, rows, half = left.shape
-    span = 2 * tiles * (rows // peers) + TAIL
+                target_rows = pl.ds(pl.multiple_of(at + tile * piece, TAIL), piece)
+                out[:, target_rows, :] = ref[tile].reshape(peers, piece, half)
+            return carry
+
+        lax.fori_loop(0, tiles, one_tile, 0)
+        for peer in range(peers):
+            out[peer, tail_at:, :] = tail
+
     return pl.pallas_call(
-        pack_body,
-        in_specs=[in_memory()] * 3,
-        out_specs=in_memory(),
-        out_shape=jax.ShapeDtypeStruct((peers, span, half), BF16),
-        scratch_shapes=[pltpu.SemaphoreType.DMA],
+        body,
+        in_specs=[on_chip()] * 5,
+        out_specs=on_chip(),
+        out_shape=jax.ShapeDtypeStruct((peers, tail_at + TAIL, half), BF16),
+        scratch_shapes=[pltpu.VMEM((TAIL, half), jnp.int32)],
         name="pack",
-    )(left, right, meta)
-
-
-def pick_body(tiles, meta, pieces, out, named_by, done):
-    peers, span, _ = pieces.shape
-    piece = (span - TAIL) // (2 * tiles)
-    slots = out.shape[1] // (2 * piece)
-
-    def one_peer(peer, carry):
-        for s in range(slots):
-            slot = meta[peer, 2 * tiles + s]
-            owner, place = slot // tiles, slot % tiles
-            for at, to in ((0, 0), (tiles * piece, slots * piece)):
-                source = pl.ds(pl.multiple_of(at + place * piece, TAIL), piece)
-                pltpu.make_async_copy(
-                    pieces.at[owner, source], out.at[peer, pl.ds(to + s * piece, piece)], done
-                ).start()
-        return carry
-
-    lax.fori_loop(0, peers, one_peer, 0)
-
-    def clear(tile, carry):
-        named_by[tile] = -1
-        return carry
-
-    lax.fori_loop(0, peers * tiles, clear, 0, unroll=8)
-
-    def note(peer, carry):
-        for s in range(slots):
-            named_by[meta[peer, 2 * tiles + s]] = peer * slots + s
-        return carry
-
-    lax.fori_loop(0, peers, note, 0)
-    pltpu.make_async_copy(out, out, done).wait()
+    )(left, right, rank, target, slot)
 
 
 def pick(meta, pieces, tiles, slots):
     peers, span, half = pieces.shape
     piece = (span - TAIL) // (2 * tiles)
 
-    def body(*refs):
-        pick_body(tiles, *refs)
+    def body(meta, pieces, out, named_by):
+        def clear(tile, carry):
+            named_by[tile] = -1
+            return carry
+
+        lax.fori_loop(0, peers * tiles, clear, 0, unroll=8)
+
+        def one_peer(peer, carry):
+            for s in range(slots):
+                slot = meta[peer, 2 * tiles + s]
+                named_by[slot] = peer * slots + s
+                owner, place = slot // tiles, slot % tiles
+                for at, to in ((0, 0), (tiles * piece, slots * piece)):
+                    source = pl.ds(pl.multiple_of(at + place * piece, TAIL), piece)
+                    out[peer, to + s * piece : to + (s + 1) * piece, :] = pieces[owner, source, :]
+            return carry
+
+        lax.fori_loop(0, peers, one_peer, 0)
 
     return pl.pallas_call(
         body,
-        in_specs=[pl.BlockSpec(memory_space=pltpu.SMEM), in_memory()],
-        out_specs=[in_memory(), pl.BlockSpec(memory_space=pltpu.SMEM)],
+        in_specs=[scalars(), on_chip()],
+        out_specs=[on_chip(), scalars()],
         out_shape=[
             jax.ShapeDtypeStruct((peers, 2 * slots * piece, half), BF16),
             jax.ShapeDtypeStruct((peers * tiles,), jnp.int32),
         ],
-        scratch_shapes=[pltpu.SemaphoreType.DMA],
         name="pick",
     )(meta, pieces)
 
 
 def place_body(tiles, meta, named_by, fresh, old, out, sums):
     peers, span, half = fresh.shape
-    piece = old.shape[1] // tiles
+    piece = (old.shape[1] - TAIL) // (2 * tiles)
     slots = span // piece
     lane = lax.broadcasted_iota(jnp.int32, (piece, half), 1)
 
@@ -315,22 +296,12 @@
 
     return pl.pallas_call(
         body,
-        grid=(1,),
-        in_specs=[
-            pl.BlockSpec(memory_space=pltpu.SMEM),
-            pl.BlockSpec(memory_space=pltpu.SMEM),
-            pl.BlockSpec(fresh.shape, lambda g: (0, 0, 0)),
-            pl.BlockSpec((peers, tiles * piece, half), lambda g: (0, 0, 0)),
-        ],
-        out_specs=[
-            pl.BlockSpec((peers, tiles * piece + TAIL, half), lambda g: (0, 0, 0)),
-            pl.BlockSpec((8, half), lambda g: (0, 0)),
-        ],
+        in_specs=[scalars(), scalars(), on_chip(), on_chip()],
+        out_specs=[on_chip(), on_chip()],
         out_shape=[
             jax.ShapeDtypeStruct((peers, tiles * piece + TAIL, half), BF16),
             jax.ShapeDtypeStruct((8, half), F32),
         ],
-        compiler_params=pltpu.CompilerParams(vmem_limit_bytes=60 * 2**20),
         name="place",
     )(meta, named_by, fresh, pieces)
 
@@ -353,15 +324,15 @@
     tiles, rows, half = current_left.shape[1:]
     slots = owner_slot.shape[1]
     piece = rows // peers
-    table = jnp.concatenate([current_rank, target_rank, owner_slot], axis=1).astype(BF16)
-    table = jnp.pad(table, ((0, TAIL - 1), (0, half - table.shape[1])))
-    pieces = exchange(pack(current_left[0], current_right[0], table, peers), "col")
+    packed = pack(
+        current_left[0], current_right[0], current_rank, target_rank, owner_slot, peers
+    )
+    pieces = exchange(packed, "col")
     meta = pieces[:, 2 * tiles * piece, :].astype(jnp.int32)
     own = jnp.concatenate([owner_slot, update_rank], axis=0)
-    width = jnp.full((1,), tiles, jnp.int32)
     chosen, named_by = pick(meta, pieces, tiles, slots)
     arrived = exchange(chosen, "col")
-    fresh, returned_right = recompress(meta, own, width, arrived, update_left[0], update_right[0])
+    fresh, returned_right = recompress(meta, own, tiles, arrived, update_left[0], update_right[0])
     fresh = exchange(fresh, "col")
     placed, sums = place(meta, named_by, fresh, pieces, tiles)
     placed = exchange(placed, "col")

time: 552 us -> 272 us (0.49)
  Pallas kernels: 332 us -> 55 us
    pallas_call x4, Pallas kernels: 332 us -> 55 us  [the longest x1 35.8 us: recompress(): pl.pallas_call(body, in_specs=[scalars(), scalars(), on_chip(), on_chip()...]
where the time goes in v2:
time: 272 us
  blocking collectives  146 us (54%)
  Pallas kernels  55 us (20%)
  waiting for transfers between devices  44.6 us (16%)
  starting transfers between devices  13.1 us (5%)
  local copies, waits for them, and re-layouts  9.3 us (3%)
    all_to_all x3, blocking collectives, exchange(): return lax.all_to_all(value, axis, split_axis=0, concat_axis=0, tiled=True)  146 us
    all_to_all x2, waiting for transfers between devices, exchange(): return lax.all_to_all(value, axis, split_axis=0, concat_axis=0, tiled=True)  44.6 us
    pallas_call x1, Pallas kernels, recompress(): pl.pallas_call(body, in_specs=[scalars(), scalars(), on_chip(), on_chip()...  35.8 us
    all_to_all x2, starting transfers between devices, exchange(): return lax.all_to_all(value, axis, split_axis=0, concat_axis=0, tiled=True)  13.1 us
    pallas_call x1, Pallas kernels, place(): pl.pallas_call(body, in_specs=[scalars(), scalars(), on_chip(), on_chip()...  6.99 us
    pallas_call x1, Pallas kernels, pack(): pl.pallas_call(body, in_specs=[on_chip()] * 5, out_specs=on_chip(), out_s...  6.08 us
    pallas_call x1, Pallas kernels, pick(): pl.pallas_call(body, in_specs=[scalars(), on_chip()], out_specs=[on_chip(...  6.07 us
  transfers between devices with their start and end apart: 2, of which 2 were waited for; matrix products, arithmetic and copies ran while one was open for 1% of the time, Pallas kernels for 0%

profile of v2, /device:TPU:1, one launch (start us, length us, event | category | flops | bytes accessed | tf_op | source)
XLA Modules:
  0.0 271.6 jit_solution(14449914596741113088)
XLA Ops:
  0.6 6.1 %pack.1 = bf16[16,1552,128]{2,1,0:T(8,128)(2,1)} custom-call(bf16[16,768,128]{2,1,0:T(8,128)(2,1)} %bitcast.15, bf16[16,768,128]{2,1,0:T(8,128)(2,1)} %bitcast.16, s32[1,16]{1,0:T(1,128)} %rank.1, s32[1,16]{1,0:T(1,128)} %target.1, s32[1,8]{1,0:T(1,128)} %slot.1), custom_call_target="tpu_custom_call" | custom-call | tf_op jit(solution)/shard_map/pack/pallas_call | solution.py:204
  6.7 81.5 %all_to_all.25.pieces.refs_3_ = bf16[16,1552,128]{2,1,0:T(8,128)(2,1)S(1)} all-to-all(bf16[16,1552,128]{2,1,0:T(8,128)(2,1)} %pack.1), channel_id=1, replica_groups=mesh['row'=8,'col'=16] {'col'}, dimensions={0} | all-to-all | bytes 12713984 | tf_op jit(solution)/shard_map/all_to_all | solution.py:310
  88.2 0.0 copy-start
  88.2 2.7 copy-done
  90.9 0.6 slice_convert_fusion.1
  91.5 6.1 %pick.1 = (bf16[16,768,128]{2,1,0:T(8,128)(2,1)}, s32[256]{0:T(256)}) custom-call(s32[16,128]{1,0:T(8,128)} %bitcast.20, bf16[16,1552,128]{2,1,0:T(8,128)(2,1)} %copy-done), custom_call_target="tpu_custom_call" | custom-call | tf_op jit(solution)/shard_map/pick/pallas_call | solution.py:237
  97.6 0.0 copy-start.2
  97.6 0.0 copy-start.3
  97.6 3.8 %all-to-all-start.1 = ((bf16[16,768,128]{2,1,0:T(8,128)(2,1)}), bf16[16,768,128]{2,1,0:T(8,128)(2,1)S(1)}, u32[]{:S(2)}, u32[]{:S(2)}) async-start(bf16[16,768,128]{2,1,0:T(8,128)(2,1)} %get-tuple-element.9), calls=%async_computation.1 | async-start | bytes 6291456 | tf_op jit(solution)/shard_map/all_to_all | solution.py:310
  101.4 0.0 copy-done.2
  101.4 0.0 copy-done.3
  101.4 0.6 pad_add_fusion.own
  102.0 43.1 %all-to-all-done.1.arrived = bf16[16,768,128]{2,1,0:T(8,128)(2,1)S(1)} async-done(((bf16[16,768,128]{2,1,0:T(8,128)(2,1)}), bf16[16,768,128]{2,1,0:T(8,128)(2,1)S(1)}, u32[]{:S(2)}, u32[]{:S(2)}) %all-to-all-start.1) | async-done | bytes 3145760 | tf_op jit(solution)/shard_map/all_to_all | solution.py:310
  145.1 0.0 copy-start.1
  145.1 1.7 copy-done.1
  146.7 35.8 %recompress.1 = (bf16[16,384,128]{2,1,0:T(8,128)(2,1)}, bf16[8,768,128]{2,1,0:T(8,128)(2,1)}) custom-call(s32[16,128]{1,0:T(8,128)} %bitcast.21, s32[2,8]{1,0:T(2,128)} %pad_add_fusion.own, bf16[16,768,128]{2,1,0:T(8,128)(2,1)} %copy-done.1, bf16[8,768,128]{2,1,0:T(8,128)(2,1)} %bitcast.17, bf16[8,768,128]{2,1,0:T(8,128)(2,1)} %bitcast.18), custom_call_target="tpu_custom_call" | custom-call | tf_op jit(solution)/shard_map/recompress/pallas_call | solution.py:167
  182.5 24.1 %all_to_all.26.refs_2_ = bf16[16,384,128]{2,1,0:T(8,128)(2,1)} all-to-all(bf16[16,384,128]{2,1,0:T(8,128)(2,1)} %get-tuple-element.10), channel_id=1, replica_groups=mesh['row'=8,'col'=16] {'col'}, dimensions={0} | all-to-all | bytes 3145728 | tf_op jit(solution)/shard_map/all_to_all | solution.py:310
  206.6 7.0 %place.1 = (bf16[16,784,128]{2,1,0:T(8,128)(2,1)}, f32[8,128]{1,0:T(8,128)}) custom-call(s32[16,128]{1,0:T(8,128)} %bitcast.22, s32[256]{0:T(256)} %get-tuple-element.8.refs_1_, bf16[16,384,128]{2,1,0:T(8,128)(2,1)} %all_to_all.26.refs_2_, bf16[16,1552,128]{2,1,0:T(8,128)(2,1)} %copy-done), custom_call_target="tpu_custom_call" | custom-call | tf_op jit(solution)/shard_map/place/pallas_call | solution.py:297
  213.6 40.1 %all_to_all.27 = bf16[16,784,128]{2,1,0:T(8,128)(2,1)S(1)} all-to-all(bf16[16,784,128]{2,1,0:T(8,128)(2,1)} %get-tuple-element.11), channel_id=1, replica_groups=mesh['row'=8,'col'=16] {'col'}, dimensions={0} | all-to-all | bytes 6422528 | tf_op jit(solution)/shard_map/all_to_all | solution.py:310
  253.8 0.6 fusion
  254.4 1.2 broadcast_in_dim.7
  255.6 9.4 %all-to-all-start.4 = ((f32[8,1,1]{2,1,0:T(1,128)}), f32[8,1,1]{2,1,0:T(1,128)S(1)}, u32[]{:S(2)}, u32[]{:S(2)}) async-start(f32[8,1,1]{2,1,0:T(1,128)} %broadcast_in_dim.7), calls=%async_computation.4 | async-start | bytes 8192 | tf_op jit(solution)/shard_map/all_to_all | solution.py:310
  265.0 0.3 slice.13
  265.3 2.5 copy.20
  267.8 0.2 copy.21
  268.0 1.5 all-to-all-done.4
  269.5 0.6 reduce_sum.29
  270.9 0.7 sqrt.11
  (4 shorter events, 0.1 us)
Async XLA Ops:
  88.2 2.7 copy-start
  97.6 3.8 %copy-start.2 = (s32[1,8]{1,0:T(1,128)S(1)}, s32[1,8]{1,0:T(1,128)}, u32[]{:S(2)}) copy-start(s32[1,8]{1,0:T(1,128)} %slot.1) | copy-start | bytes 100
  97.6 3.8 %copy-start.3 = (s32[1,8]{1,0:T(1,128)S(1)}, s32[1,8]{1,0:T(1,128)}, u32[]{:S(2)}) copy-start(s32[1,8]{1,0:T(1,128)} %param.14) | copy-start | bytes 100
  97.6 47.4 %all-to-all-start.1 = ((bf16[16,768,128]{2,1,0:T(8,128)(2,1)}), bf16[16,768,128]{2,1,0:T(8,128)(2,1)S(1)}, u32[]{:S(2)}, u32[]{:S(2)}) async-start(bf16[16,768,128]{2,1,0:T(8,128)(2,1)} %get-tuple-element.9), calls=%async_computation.1 | async-start | bytes 6291456 | tf_op jit(solution)/shard_map/all_to_all | solution.py:310
  145.1 1.7 copy-start.1
  255.6 13.9 %all-to-all-start.4 = ((f32[8,1,1]{2,1,0:T(1,128)}), f32[8,1,1]{2,1,0:T(1,128)S(1)}, u32[]{:S(2)}, u32[]{:S(2)}) async-start(f32[8,1,1]{2,1,0:T(1,128)} %broadcast_in_dim.7), calls=%async_computation.4 | async-start | bytes 8192 | tf_op jit(solution)/shard_map/all_to_all | solution.py:310
